TPU v7x, 32 devices: a whole 2x2x4 slice. The times are simulated.
32 devices in a mesh: section: 4 (over z), expert: 8 (over y, x, core).
Axes of the slice: x: 2, y: 2, z: 4, core: 2. Of those that a mesh axis runs over, the one named last changes fastest.
Arguments:
- tokens: bfloat16 [4, 1, 128, 1024], P(None, None, 'expert'), may hold values from -6 to 6
- expert_ids: int32 [4, 4, 1, 128, 2], P('section', None, None, 'expert'), may hold values from 0 to 7, as said below
- router_weight: float32 [4, 1, 1024, 8], P('section'), may hold values from -0.375 to 0.375
- w_gate: bfloat16 [4, 8, 1024, 1792], P('section', 'expert'), may hold values from -0.1875 to 0.1875
- w_up: bfloat16 [4, 8, 1024, 1792], P('section', 'expert'), may hold values from -0.1875 to 0.1875
- w_down: bfloat16 [4, 8, 1792, 1024], P('section', 'expert'), may hold values from -0.125 to 0.125
Outputs:
- layer_outputs: bfloat16 [4, 4, 1, 128, 1024], P('section', None, None, 'expert')
Inputs may be any that keep to these rules, and one draw needn't show every extreme that they name: `expert_ids`: the two entries of a token are different experts. In each aligned block of 8 tokens (same layer, micro-batch and replica) no expert is named by more than 4 tokens, and some expert by exactly 4.
All inputs are finite; a program needn't handle non-finite values.
Results may differ from a plain program's by a relative error of at most 0.02.
Values may be sent and summed in bfloat16 or wider, within the bound.
No kernel may reach another device: no remote copies, remote signals or barrier semaphores. Data moves between devices by JAX's collectives and lax.ppermute only.
A program may use at most 64 MiB of HBM per device.

v0:
```python
import jax
import jax.numpy as jnp
from jax import lax
from jax.sharding import PartitionSpec as P

EXPERTS = 8
CAP = 4


def shifted(array, axis, by):
    peers = lax.axis_size(axis)
    pairs = [(i, i + by) for i in range(peers) if 0 <= i + by < peers]
    return lax.ppermute(array, axis, pairs)


def prepare(current, routes, router_mat, capacity):
    replicas, tok_rows, width = current.shape
    values = current.astype(jnp.float32)
    normed = (values * lax.rsqrt(jnp.mean(values * values, axis=-1, keepdims=True) + 1e-06)).astype(
        jnp.bfloat16
    )
    logits = jnp.einsum(
        "rtd,rde->rte", normed.astype(jnp.float32), router_mat, precision=lax.Precision.HIGHEST
    )
    scores = jax.nn.sigmoid(logits)
    expert_range = jnp.arange(EXPERTS, dtype=jnp.int32)
    matches = routes[..., None] == expert_range
    picked = jnp.sum(jnp.where(matches, scores[:, :, None, :], 0.0), axis=-1)
    gates = picked / jnp.sum(picked, axis=-1, keepdims=True)
    flat_ids = routes.reshape(replicas, tok_rows * 2)
    one_hot = (flat_ids[..., None] == expert_range).astype(jnp.int32)
    earlier = jnp.cumsum(one_hot, axis=1) - one_hot
    position = jnp.sum(earlier * one_hot, axis=-1)
    target = flat_ids * capacity + position
    slot_range = jnp.arange(EXPERTS * capacity, dtype=jnp.int32)
    placing = jnp.sum(
        (
            target.reshape(replicas, tok_rows, 2)[:, None, :, :] == slot_range[None, :, None, None]
        ).astype(jnp.int32),
        axis=-1,
    ).astype(jnp.bfloat16)
    outgoing = jnp.einsum(
        "rst,rtd->rsd", placing, normed, preferred_element_type=jnp.float32
    ).astype(jnp.bfloat16)
    outgoing = outgoing.reshape(replicas * EXPERTS, capacity, width)
    return (gates, target, outgoing)


def compute(received, weights, active_flag):
    gate_mat, up_mat, down_mat = weights
    width = received.shape[2]
    total_rows = received.shape[0] * received.shape[1]
    flat_rows = received.reshape(total_rows, width)

    def working(inputs):
        gate_val = jnp.dot(inputs, gate_mat, preferred_element_type=jnp.float32)
        up_val = jnp.dot(inputs, up_mat, preferred_element_type=jnp.float32)
        inner = (jax.nn.silu(gate_val) * up_val).astype(jnp.bfloat16)
        return jnp.dot(inner, down_mat, preferred_element_type=jnp.float32).astype(jnp.bfloat16)

    def resting(inputs):
        return jnp.zeros((total_rows, width), jnp.bfloat16)

    return lax.cond(active_flag, working, resting, flat_rows).reshape(received.shape)


def send_out(outgoing, serve):
    return serve(lax.all_to_all(outgoing, "expert", split_axis=0, concat_axis=0, tiled=True))


def combine(current, gates, target, answers, capacity):
    replicas, tok_rows, width = current.shape
    values = current.astype(jnp.float32)
    answers = answers.reshape(replicas, EXPERTS * capacity, width)
    gathered = answers[jnp.arange(replicas, dtype=jnp.int32)[:, None], target]
    weighted = gathered.reshape(replicas, tok_rows, 2, width).astype(jnp.float32) * gates[..., None]
    return (values + jnp.sum(weighted, axis=2)).astype(jnp.bfloat16)


def per_device(tokens, expert_ids, router_weight, w_gate, w_up, w_down):
    batches, replicas, tok_dev, width = tokens.shape
    section_count = lax.axis_size("section")
    section_index = lax.axis_index("section")
    pieces = 1
    capacity = 2 * CAP
    tok_rows = tok_dev // pieces
    unit_total = batches * pieces
    weights = (w_gate[0, 0], w_up[0, 0], w_down[0, 0])
    router_mat = router_weight[0]
    routes_all = expert_ids[0]
    zero_index = jnp.zeros((), jnp.int32)

    def locate(unit_now):
        clipped = jnp.clip(unit_now, 0, unit_total - 1)
        batch_now = clipped // pieces
        offset = clipped % pieces * tok_rows
        return (batch_now, offset)

    def store_rows(stored, result, unit_now):
        valid = jnp.logical_and(unit_now >= 0, unit_now < unit_total)
        batch_now, offset = locate(unit_now)
        updated = lax.dynamic_update_slice(
            stored, result[None], (batch_now, zero_index, offset, zero_index)
        )
        return jnp.where(valid, updated, stored)

    def inputs_for(unit_now):
        batch_now, offset = locate(unit_now)
        fresh = lax.dynamic_slice(
            tokens, (batch_now, zero_index, offset, zero_index), (1, replicas, tok_rows, width)
        )[0]
        routes = lax.dynamic_slice(
            routes_all, (batch_now, zero_index, offset, zero_index), (1, replicas, tok_rows, 2)
        )[0]
        return (fresh, routes)

    stored_start = jnp.zeros((batches, replicas, tok_dev, width), jnp.bfloat16)

    def advance(step_now, carry):
        previous, stored = carry
        incoming = shifted(previous, "section", 1)
        unit_now = step_now - section_index
        active_flag = jnp.logical_and(unit_now >= 0, unit_now < unit_total)
        fresh, routes = inputs_for(unit_now)
        current = jnp.where(section_index == 0, fresh, incoming)
        gates, target, outgoing = prepare(current, routes, router_mat, capacity)

        def serve(received):
            results = compute(received, weights, active_flag)
            return lax.all_to_all(results, "expert", split_axis=0, concat_axis=0, tiled=True)

        answers = send_out(outgoing, serve)
        result = combine(current, gates, target, answers, capacity)
        return (result, store_rows(stored, result, unit_now))

    start = (jnp.zeros((replicas, tok_rows, width), jnp.bfloat16), stored_start)
    finished = lax.fori_loop(0, unit_total + section_count - 1, advance, start)
    return finished[1][None]


def solution(mesh):
    in_specs = (
        P(None, None, "expert", None),
        P("section", None, None, "expert", None),
        P("section", None, None, None),
        P("section", "expert", None, None),
        P("section", "expert", None, None),
        P("section", "expert", None, None),
    )
    out_specs = P("section", None, None, "expert", None)
    return jax.shard_map(
        per_device, mesh=mesh, in_specs=in_specs, out_specs=out_specs, check_vma=False
    )
```

profile of v0, /device:TPU:24, one launch (start us, length us, event | category | flops | bytes accessed | tf_op | source)
XLA Modules:
  0.0 236.8 jit_solution(14829322959485642125)
XLA Ops:
  0.0 236.1 %while.18 = (s32[]{:T(128)}, bf16[1,16,1024]{2,1,0:T(8,128)(2,1)S(1)}, bf16[4,1,16,1024]{3,2,1,0:T(8,128)(2,1)S(1)}, pred[]{:T(512)}, s32[]{:T(128)}, /*index=5*...) while((s32[]{:T(128)}, ...), condition=%wide.region_10.11_spmd.clone, body=%wide.region_0.10_spmd.clone.sunk | while | flops 709444864 | bytes 14371643 | solution.py:137
  12.4 4.5 %all-to-all-done = bf16[8,8,1024]{2,1,0:T(8,128)(2,1)S(1)} async-done(((bf16[8,8,1024]{2,1,0:T(8,128)(2,1)}), bf16[8,8,1024]{2,1,0:T(8,128)(2,1)S(1)}, u32[]{:S(2)}, u32[]{:S(2)}) %all-to-all-start) | async-done | bytes 131104 | tf_op jit(solution)/shard_map/while/body/eval_jaxpr/all_to_all | solution.py:68
  21.0 5.3 %all-to-all-done.1 = bf16[8,8,1024]{2,1,0:T(8,128)(2,1)S(1)} async-done(((bf16[8,8,1024]{2,1,0:T(8,128)(2,1)}), bf16[8,8,1024]{2,1,0:T(8,128)(2,1)S(1)}, u32[]{:S(2)}, u32[]{:S(2)}) %all-to-all-start.1) | async-done | bytes 131104 | tf_op jit(solution)/shard_map/while/body/eval_jaxpr/all_to_all | solution.py:130
  39.5 4.4 %all-to-all-done = bf16[8,8,1024]{2,1,0:T(8,128)(2,1)S(1)} async-done(((bf16[8,8,1024]{2,1,0:T(8,128)(2,1)}), bf16[8,8,1024]{2,1,0:T(8,128)(2,1)S(1)}, u32[]{:S(2)}, u32[]{:S(2)}) %all-to-all-start) | async-done | bytes 131104 | tf_op jit(solution)/shard_map/while/body/eval_jaxpr/all_to_all | solution.py:68
  48.1 5.3 %all-to-all-done.1 = bf16[8,8,1024]{2,1,0:T(8,128)(2,1)S(1)} async-done(((bf16[8,8,1024]{2,1,0:T(8,128)(2,1)}), bf16[8,8,1024]{2,1,0:T(8,128)(2,1)S(1)}, u32[]{:S(2)}, u32[]{:S(2)}) %all-to-all-start.1) | async-done | bytes 131104 | tf_op jit(solution)/shard_map/while/body/eval_jaxpr/all_to_all | solution.py:130
  66.6 4.4 %all-to-all-done = bf16[8,8,1024]{2,1,0:T(8,128)(2,1)S(1)} async-done(((bf16[8,8,1024]{2,1,0:T(8,128)(2,1)}), bf16[8,8,1024]{2,1,0:T(8,128)(2,1)S(1)}, u32[]{:S(2)}, u32[]{:S(2)}) %all-to-all-start) | async-done | bytes 131104 | tf_op jit(solution)/shard_map/while/body/eval_jaxpr/all_to_all | solution.py:68
  75.2 5.3 %all-to-all-done.1 = bf16[8,8,1024]{2,1,0:T(8,128)(2,1)S(1)} async-done(((bf16[8,8,1024]{2,1,0:T(8,128)(2,1)}), bf16[8,8,1024]{2,1,0:T(8,128)(2,1)S(1)}, u32[]{:S(2)}, u32[]{:S(2)}) %all-to-all-start.1) | async-done | bytes 131104 | tf_op jit(solution)/shard_map/while/body/eval_jaxpr/all_to_all | solution.py:130
  85.2 19.0 %collective-permute-done = bf16[1,16,1024]{2,1,0:T(8,128)(2,1)S(1)} collective-permute-done((bf16[1,16,1024]{2,1,0:T(8,128)(2,1)S(1)}, bf16[1,16,1024]{2,1,0:T(8,128)(2,1)S(1)}, u32[]{:S(2)}, u32[]{:S(2)}) %collective-permute-start) | collective-permute-done | bytes 32800 | tf_op jit(solution)/shard_map/while/body/eval_jaxpr/ppermute | solution.py:13
  110.4 4.4 %all-to-all-done = bf16[8,8,1024]{2,1,0:T(8,128)(2,1)S(1)} async-done(((bf16[8,8,1024]{2,1,0:T(8,128)(2,1)}), bf16[8,8,1024]{2,1,0:T(8,128)(2,1)S(1)}, u32[]{:S(2)}, u32[]{:S(2)}) %all-to-all-start) | async-done | bytes 131104 | tf_op jit(solution)/shard_map/while/body/eval_jaxpr/all_to_all | solution.py:68
  114.8 8.0 %conditional.3 = (bf16[64,1024]{1,0:T(8,128)(2,1)}) conditional(s32[]{:T(128)} %convert_element_type.215, () %tuple.65, (bf16[8,8,1024]{2,1,0:T(8,128)(2,1)S(1)}, bf16[1024,1792]{1,0:T(8,128)(2,1)}, bf16[1024,1792]{1,0:T(8,128)(2,1)}, bf16[1792,1024]{1,0:T(8,128)(2,1)}) %tuple.66), branch_computations={%region_5.5_spmd, %region_6.6_spmd} | conditional | flops 705396736 | bytes 12320776 | solution.py:64
  117.6 5.2 %fusion.2 = bf16[64,1024]{1,0:T(8,128)(2,1)} fusion(bf16[1792,1024]{1,0:T(8,128)(2,1)} %get-tuple-element.264, bf16[1024,1792]{1,0:T(8,128)(2,1)} %get-tuple-element.263, f32[64,1792]{1,0:T(8,128)S(1)} %fusion.11, bf16[8,8,1024]{2,1,0:T(8,128)(2,1)S(1)} %get-tuple-element.261), kind=kOutput, calls=%fused_computation.4 | convolution fusion | flops 470515712 | bytes 8060928 | tf_op jit(solution)/shard_map/while/body/eval_jaxpr/cond/branch_1_fun/dot_general | solution.py:59
  126.3 5.3 %all-to-all-done.1 = bf16[8,8,1024]{2,1,0:T(8,128)(2,1)S(1)} async-done(((bf16[8,8,1024]{2,1,0:T(8,128)(2,1)}), bf16[8,8,1024]{2,1,0:T(8,128)(2,1)S(1)}, u32[]{:S(2)}, u32[]{:S(2)}) %all-to-all-start.1) | async-done | bytes 131104 | tf_op jit(solution)/shard_map/while/body/eval_jaxpr/all_to_all | solution.py:130
  144.8 4.4 %all-to-all-done = bf16[8,8,1024]{2,1,0:T(8,128)(2,1)S(1)} async-done(((bf16[8,8,1024]{2,1,0:T(8,128)(2,1)}), bf16[8,8,1024]{2,1,0:T(8,128)(2,1)S(1)}, u32[]{:S(2)}, u32[]{:S(2)}) %all-to-all-start) | async-done | bytes 131104 | tf_op jit(solution)/shard_map/while/body/eval_jaxpr/all_to_all | solution.py:68
  149.3 8.0 %conditional.3 = (bf16[64,1024]{1,0:T(8,128)(2,1)}) conditional(s32[]{:T(128)} %convert_element_type.215, () %tuple.65, (bf16[8,8,1024]{2,1,0:T(8,128)(2,1)S(1)}, bf16[1024,1792]{1,0:T(8,128)(2,1)}, bf16[1024,1792]{1,0:T(8,128)(2,1)}, bf16[1792,1024]{1,0:T(8,128)(2,1)}) %tuple.66), branch_computations={%region_5.5_spmd, %region_6.6_spmd} | conditional | flops 705396736 | bytes 12320776 | solution.py:64
  152.0 5.2 %fusion.2 = bf16[64,1024]{1,0:T(8,128)(2,1)} fusion(bf16[1792,1024]{1,0:T(8,128)(2,1)} %get-tuple-element.264, bf16[1024,1792]{1,0:T(8,128)(2,1)} %get-tuple-element.263, f32[64,1792]{1,0:T(8,128)S(1)} %fusion.11, bf16[8,8,1024]{2,1,0:T(8,128)(2,1)S(1)} %get-tuple-element.261), kind=kOutput, calls=%fused_computation.4 | convolution fusion | flops 470515712 | bytes 8060928 | tf_op jit(solution)/shard_map/while/body/eval_jaxpr/cond/branch_1_fun/dot_general | solution.py:59
  160.8 5.3 %all-to-all-done.1 = bf16[8,8,1024]{2,1,0:T(8,128)(2,1)S(1)} async-done(((bf16[8,8,1024]{2,1,0:T(8,128)(2,1)}), bf16[8,8,1024]{2,1,0:T(8,128)(2,1)S(1)}, u32[]{:S(2)}, u32[]{:S(2)}) %all-to-all-start.1) | async-done | bytes 131104 | tf_op jit(solution)/shard_map/while/body/eval_jaxpr/all_to_all | solution.py:130
  179.3 4.4 %all-to-all-done = bf16[8,8,1024]{2,1,0:T(8,128)(2,1)S(1)} async-done(((bf16[8,8,1024]{2,1,0:T(8,128)(2,1)}), bf16[8,8,1024]{2,1,0:T(8,128)(2,1)S(1)}, u32[]{:S(2)}, u32[]{:S(2)}) %all-to-all-start) | async-done | bytes 131104 | tf_op jit(solution)/shard_map/while/body/eval_jaxpr/all_to_all | solution.py:68
  183.7 8.0 %conditional.3 = (bf16[64,1024]{1,0:T(8,128)(2,1)}) conditional(s32[]{:T(128)} %convert_element_type.215, () %tuple.65, (bf16[8,8,1024]{2,1,0:T(8,128)(2,1)S(1)}, bf16[1024,1792]{1,0:T(8,128)(2,1)}, bf16[1024,1792]{1,0:T(8,128)(2,1)}, bf16[1792,1024]{1,0:T(8,128)(2,1)}) %tuple.66), branch_computations={%region_5.5_spmd, %region_6.6_spmd} | conditional | flops 705396736 | bytes 12320776 | solution.py:64
  186.5 5.2 %fusion.2 = bf16[64,1024]{1,0:T(8,128)(2,1)} fusion(bf16[1792,1024]{1,0:T(8,128)(2,1)} %get-tuple-element.264, bf16[1024,1792]{1,0:T(8,128)(2,1)} %get-tuple-element.263, f32[64,1792]{1,0:T(8,128)S(1)} %fusion.11, bf16[8,8,1024]{2,1,0:T(8,128)(2,1)S(1)} %get-tuple-element.261), kind=kOutput, calls=%fused_computation.4 | convolution fusion | flops 470515712 | bytes 8060928 | tf_op jit(solution)/shard_map/while/body/eval_jaxpr/cond/branch_1_fun/dot_general | solution.py:59
  195.2 5.3 %all-to-all-done.1 = bf16[8,8,1024]{2,1,0:T(8,128)(2,1)S(1)} async-done(((bf16[8,8,1024]{2,1,0:T(8,128)(2,1)}), bf16[8,8,1024]{2,1,0:T(8,128)(2,1)S(1)}, u32[]{:S(2)}, u32[]{:S(2)}) %all-to-all-start.1) | async-done | bytes 131104 | tf_op jit(solution)/shard_map/while/body/eval_jaxpr/all_to_all | solution.py:130
  213.7 4.4 %all-to-all-done = bf16[8,8,1024]{2,1,0:T(8,128)(2,1)S(1)} async-done(((bf16[8,8,1024]{2,1,0:T(8,128)(2,1)}), bf16[8,8,1024]{2,1,0:T(8,128)(2,1)S(1)}, u32[]{:S(2)}, u32[]{:S(2)}) %all-to-all-start) | async-done | bytes 131104 | tf_op jit(solution)/shard_map/while/body/eval_jaxpr/all_to_all | solution.py:68
  218.1 8.0 %conditional.3 = (bf16[64,1024]{1,0:T(8,128)(2,1)}) conditional(s32[]{:T(128)} %convert_element_type.215, () %tuple.65, (bf16[8,8,1024]{2,1,0:T(8,128)(2,1)S(1)}, bf16[1024,1792]{1,0:T(8,128)(2,1)}, bf16[1024,1792]{1,0:T(8,128)(2,1)}, bf16[1792,1024]{1,0:T(8,128)(2,1)}) %tuple.66), branch_computations={%region_5.5_spmd, %region_6.6_spmd} | conditional | flops 705396736 | bytes 12320776 | solution.py:64
  220.9 5.2 %fusion.2 = bf16[64,1024]{1,0:T(8,128)(2,1)} fusion(bf16[1792,1024]{1,0:T(8,128)(2,1)} %get-tuple-element.264, bf16[1024,1792]{1,0:T(8,128)(2,1)} %get-tuple-element.263, f32[64,1792]{1,0:T(8,128)S(1)} %fusion.11, bf16[8,8,1024]{2,1,0:T(8,128)(2,1)S(1)} %get-tuple-element.261), kind=kOutput, calls=%fused_computation.4 | convolution fusion | flops 470515712 | bytes 8060928 | tf_op jit(solution)/shard_map/while/body/eval_jaxpr/cond/branch_1_fun/dot_general | solution.py:59
  229.7 5.3 %all-to-all-done.1 = bf16[8,8,1024]{2,1,0:T(8,128)(2,1)S(1)} async-done(((bf16[8,8,1024]{2,1,0:T(8,128)(2,1)}), bf16[8,8,1024]{2,1,0:T(8,128)(2,1)S(1)}, u32[]{:S(2)}, u32[]{:S(2)}) %all-to-all-start.1) | async-done | bytes 131104 | tf_op jit(solution)/shard_map/while/body/eval_jaxpr/all_to_all | solution.py:130
  (230 shorter events, 129.4 us)
Async XLA Ops:
  0.0 5.8 %collective-permute-start = (bf16[1,16,1024]{2,1,0:T(8,128)(2,1)S(1)}, bf16[1,16,1024]{2,1,0:T(8,128)(2,1)S(1)}, u32[]{:S(2)}, u32[]{:S(2)}) collective-permute-start(bf16[1,16,1024]{2,1,0:T(8,128)(2,1)S(1)} %broadcast_select_fusion.2), channel_id=1, source_target_pairs={{0,8},{8,16},{16,24},{1,9},{9,17},{17,25},{2,10},{10,18},{18,26},{... | collective-permute-start | bytes 98312 | tf_op jit(solution)/shard_map/while/body/eval_jaxpr/ppermute | solution.py:13
  7.6 9.2 %all-to-all-start = ((bf16[8,8,1024]{2,1,0:T(8,128)(2,1)}), bf16[8,8,1024]{2,1,0:T(8,128)(2,1)S(1)}, u32[]{:S(2)}, u32[]{:S(2)}) async-start(bf16[8,8,1024]{2,1,0:T(8,128)(2,1)} %fusion.50), calls=%async_computation | async-start | bytes 262144 | tf_op jit(solution)/shard_map/while/body/eval_jaxpr/all_to_all | solution.py:68
  17.5 8.8 %all-to-all-start.1 = ((bf16[8,8,1024]{2,1,0:T(8,128)(2,1)}), bf16[8,8,1024]{2,1,0:T(8,128)(2,1)S(1)}, u32[]{:S(2)}, u32[]{:S(2)}) async-start(bf16[8,8,1024]{2,1,0:T(8,128)(2,1)} %bitcast.75), calls=%async_computation.1 | async-start | bytes 262144 | tf_op jit(solution)/shard_map/while/body/eval_jaxpr/all_to_all | solution.py:130
  27.5 5.8 %collective-permute-start = (bf16[1,16,1024]{2,1,0:T(8,128)(2,1)S(1)}, bf16[1,16,1024]{2,1,0:T(8,128)(2,1)S(1)}, u32[]{:S(2)}, u32[]{:S(2)}) collective-permute-start(bf16[1,16,1024]{2,1,0:T(8,128)(2,1)S(1)} %broadcast_select_fusion.2), channel_id=1, source_target_pairs={{0,8},{8,16},{16,24},{1,9},{9,17},{17,25},{2,10},{10,18},{18,26},{... | collective-permute-start | bytes 98312 | tf_op jit(solution)/shard_map/while/body/eval_jaxpr/ppermute | solution.py:13
  35.1 8.8 %all-to-all-start = ((bf16[8,8,1024]{2,1,0:T(8,128)(2,1)}), bf16[8,8,1024]{2,1,0:T(8,128)(2,1)S(1)}, u32[]{:S(2)}, u32[]{:S(2)}) async-start(bf16[8,8,1024]{2,1,0:T(8,128)(2,1)} %fusion.50), calls=%async_computation | async-start | bytes 262144 | tf_op jit(solution)/shard_map/while/body/eval_jaxpr/all_to_all | solution.py:68
  44.6 8.8 %all-to-all-start.1 = ((bf16[8,8,1024]{2,1,0:T(8,128)(2,1)}), bf16[8,8,1024]{2,1,0:T(8,128)(2,1)S(1)}, u32[]{:S(2)}, u32[]{:S(2)}) async-start(bf16[8,8,1024]{2,1,0:T(8,128)(2,1)} %bitcast.75), calls=%async_computation.1 | async-start | bytes 262144 | tf_op jit(solution)/shard_map/while/body/eval_jaxpr/all_to_all | solution.py:130
  54.6 5.8 %collective-permute-start = (bf16[1,16,1024]{2,1,0:T(8,128)(2,1)S(1)}, bf16[1,16,1024]{2,1,0:T(8,128)(2,1)S(1)}, u32[]{:S(2)}, u32[]{:S(2)}) collective-permute-start(bf16[1,16,1024]{2,1,0:T(8,128)(2,1)S(1)} %broadcast_select_fusion.2), channel_id=1, source_target_pairs={{0,8},{8,16},{16,24},{1,9},{9,17},{17,25},{2,10},{10,18},{18,26},{... | collective-permute-start | bytes 98312 | tf_op jit(solution)/shard_map/while/body/eval_jaxpr/ppermute | solution.py:13
  62.2 8.8 %all-to-all-start = ((bf16[8,8,1024]{2,1,0:T(8,128)(2,1)}), bf16[8,8,1024]{2,1,0:T(8,128)(2,1)S(1)}, u32[]{:S(2)}, u32[]{:S(2)}) async-start(bf16[8,8,1024]{2,1,0:T(8,128)(2,1)} %fusion.50), calls=%async_computation | async-start | bytes 262144 | tf_op jit(solution)/shard_map/while/body/eval_jaxpr/all_to_all | solution.py:68
  71.7 8.8 %all-to-all-start.1 = ((bf16[8,8,1024]{2,1,0:T(8,128)(2,1)}), bf16[8,8,1024]{2,1,0:T(8,128)(2,1)S(1)}, u32[]{:S(2)}, u32[]{:S(2)}) async-start(bf16[8,8,1024]{2,1,0:T(8,128)(2,1)} %bitcast.75), calls=%async_computation.1 | async-start | bytes 262144 | tf_op jit(solution)/shard_map/while/body/eval_jaxpr/all_to_all | solution.py:130
  81.7 22.5 %collective-permute-start = (bf16[1,16,1024]{2,1,0:T(8,128)(2,1)S(1)}, bf16[1,16,1024]{2,1,0:T(8,128)(2,1)S(1)}, u32[]{:S(2)}, u32[]{:S(2)}) collective-permute-start(bf16[1,16,1024]{2,1,0:T(8,128)(2,1)S(1)} %broadcast_select_fusion.2), channel_id=1, source_target_pairs={{0,8},{8,16},{16,24},{1,9},{9,17},{17,25},{2,10},{10,18},{18,26},{... | collective-permute-start | bytes 98312 | tf_op jit(solution)/shard_map/while/body/eval_jaxpr/ppermute | solution.py:13
  106.0 8.8 %all-to-all-start = ((bf16[8,8,1024]{2,1,0:T(8,128)(2,1)}), bf16[8,8,1024]{2,1,0:T(8,128)(2,1)S(1)}, u32[]{:S(2)}, u32[]{:S(2)}) async-start(bf16[8,8,1024]{2,1,0:T(8,128)(2,1)} %fusion.50), calls=%async_computation | async-start | bytes 262144 | tf_op jit(solution)/shard_map/while/body/eval_jaxpr/all_to_all | solution.py:68
  122.9 8.8 %all-to-all-start.1 = ((bf16[8,8,1024]{2,1,0:T(8,128)(2,1)}), bf16[8,8,1024]{2,1,0:T(8,128)(2,1)S(1)}, u32[]{:S(2)}, u32[]{:S(2)}) async-start(bf16[8,8,1024]{2,1,0:T(8,128)(2,1)} %bitcast.75), calls=%async_computation.1 | async-start | bytes 262144 | tf_op jit(solution)/shard_map/while/body/eval_jaxpr/all_to_all | solution.py:130
  132.8 5.8 %collective-permute-start = (bf16[1,16,1024]{2,1,0:T(8,128)(2,1)S(1)}, bf16[1,16,1024]{2,1,0:T(8,128)(2,1)S(1)}, u32[]{:S(2)}, u32[]{:S(2)}) collective-permute-start(bf16[1,16,1024]{2,1,0:T(8,128)(2,1)S(1)} %broadcast_select_fusion.2), channel_id=1, source_target_pairs={{0,8},{8,16},{16,24},{1,9},{9,17},{17,25},{2,10},{10,18},{18,26},{... | collective-permute-start | bytes 98312 | tf_op jit(solution)/shard_map/while/body/eval_jaxpr/ppermute | solution.py:13
  140.4 8.8 %all-to-all-start = ((bf16[8,8,1024]{2,1,0:T(8,128)(2,1)}), bf16[8,8,1024]{2,1,0:T(8,128)(2,1)S(1)}, u32[]{:S(2)}, u32[]{:S(2)}) async-start(bf16[8,8,1024]{2,1,0:T(8,128)(2,1)} %fusion.50), calls=%async_computation | async-start | bytes 262144 | tf_op jit(solution)/shard_map/while/body/eval_jaxpr/all_to_all | solution.py:68
  157.3 8.8 %all-to-all-start.1 = ((bf16[8,8,1024]{2,1,0:T(8,128)(2,1)}), bf16[8,8,1024]{2,1,0:T(8,128)(2,1)S(1)}, u32[]{:S(2)}, u32[]{:S(2)}) async-start(bf16[8,8,1024]{2,1,0:T(8,128)(2,1)} %bitcast.75), calls=%async_computation.1 | async-start | bytes 262144 | tf_op jit(solution)/shard_map/while/body/eval_jaxpr/all_to_all | solution.py:130
  167.3 5.8 %collective-permute-start = (bf16[1,16,1024]{2,1,0:T(8,128)(2,1)S(1)}, bf16[1,16,1024]{2,1,0:T(8,128)(2,1)S(1)}, u32[]{:S(2)}, u32[]{:S(2)}) collective-permute-start(bf16[1,16,1024]{2,1,0:T(8,128)(2,1)S(1)} %broadcast_select_fusion.2), channel_id=1, source_target_pairs={{0,8},{8,16},{16,24},{1,9},{9,17},{17,25},{2,10},{10,18},{18,26},{... | collective-permute-start | bytes 98312 | tf_op jit(solution)/shard_map/while/body/eval_jaxpr/ppermute | solution.py:13
  174.9 8.8 %all-to-all-start = ((bf16[8,8,1024]{2,1,0:T(8,128)(2,1)}), bf16[8,8,1024]{2,1,0:T(8,128)(2,1)S(1)}, u32[]{:S(2)}, u32[]{:S(2)}) async-start(bf16[8,8,1024]{2,1,0:T(8,128)(2,1)} %fusion.50), calls=%async_computation | async-start | bytes 262144 | tf_op jit(solution)/shard_map/while/body/eval_jaxpr/all_to_all | solution.py:68
  191.7 8.8 %all-to-all-start.1 = ((bf16[8,8,1024]{2,1,0:T(8,128)(2,1)}), bf16[8,8,1024]{2,1,0:T(8,128)(2,1)S(1)}, u32[]{:S(2)}, u32[]{:S(2)}) async-start(bf16[8,8,1024]{2,1,0:T(8,128)(2,1)} %bitcast.75), calls=%async_computation.1 | async-start | bytes 262144 | tf_op jit(solution)/shard_map/while/body/eval_jaxpr/all_to_all | solution.py:130
  201.7 5.8 %collective-permute-start = (bf16[1,16,1024]{2,1,0:T(8,128)(2,1)S(1)}, bf16[1,16,1024]{2,1,0:T(8,128)(2,1)S(1)}, u32[]{:S(2)}, u32[]{:S(2)}) collective-permute-start(bf16[1,16,1024]{2,1,0:T(8,128)(2,1)S(1)} %broadcast_select_fusion.2), channel_id=1, source_target_pairs={{0,8},{8,16},{16,24},{1,9},{9,17},{17,25},{2,10},{10,18},{18,26},{... | collective-permute-start | bytes 98312 | tf_op jit(solution)/shard_map/while/body/eval_jaxpr/ppermute | solution.py:13
  209.3 8.8 %all-to-all-start = ((bf16[8,8,1024]{2,1,0:T(8,128)(2,1)}), bf16[8,8,1024]{2,1,0:T(8,128)(2,1)S(1)}, u32[]{:S(2)}, u32[]{:S(2)}) async-start(bf16[8,8,1024]{2,1,0:T(8,128)(2,1)} %fusion.50), calls=%async_computation | async-start | bytes 262144 | tf_op jit(solution)/shard_map/while/body/eval_jaxpr/all_to_all | solution.py:68
  226.2 8.8 %all-to-all-start.1 = ((bf16[8,8,1024]{2,1,0:T(8,128)(2,1)}), bf16[8,8,1024]{2,1,0:T(8,128)(2,1)S(1)}, u32[]{:S(2)}, u32[]{:S(2)}) async-start(bf16[8,8,1024]{2,1,0:T(8,128)(2,1)} %bitcast.75), calls=%async_computation.1 | async-start | bytes 262144 | tf_op jit(solution)/shard_map/while/body/eval_jaxpr/all_to_all | solution.py:130
  236.1 0.7 copy-start
where the time goes:
time: 240 us; the launch traced here: 237 us
  waiting for transfers between devices  101 us (42%)
  starting transfers between devices  56.6 us (24%)
  matrix products  45 us (19%)
  local copies, waits for them, and re-layouts  21.9 us (9%)
  other arithmetic  11.3 us (5%)
    all_to_all x7, waiting for transfers between devices, serve(): lax.all_to_all(results, 'expert', split_axis=0, concat_axis=0, tiled=True)  37.4 us
    ppermute x7, waiting for transfers between devices, shifted(): return lax.ppermute(array, axis, pairs)  32.4 us
    all_to_all x7, waiting for transfers between devices, send_out(): lax.all_to_all(outgoing, 'expert', split_axis=0, concat_axis=0, tiled=True)  31.1 us
    all_to_all x7, starting transfers between devices, send_out(): lax.all_to_all(outgoing, 'expert', split_axis=0, concat_axis=0, tiled=True)  24 us
    all_to_all x7, starting transfers between devices, serve(): lax.all_to_all(results, 'expert', split_axis=0, concat_axis=0, tiled=True)  23.6 us
    dot_general x4, matrix products, working(): jnp.dot(inner, down_mat, preferred_element_type=jnp.float32)  21 us
    dot_general x4, matrix products, working(): gate_val = jnp.dot(inputs, gate_mat, preferred_element_type=jnp.float32)  11.1 us
    ppermute x7, starting transfers between devices, shifted(): return lax.ppermute(array, axis, pairs)  9.04 us
  transfers between devices with their start and end apart: 21, of which 21 were waited for; matrix products, arithmetic and copies ran while one was open for 10% of the time, Pallas kernels for 0%

commit v1 on v0

v1 whole, which is shorter than its diff:
```python
import jax
import jax.numpy as jnp
from jax import lax
from jax.experimental import pallas as pl
from jax.experimental.pallas import tpu as pltpu
from jax.sharding import PartitionSpec as P

CAP = 4
VMEM = pl.BlockSpec(memory_space=pltpu.VMEM)
SMEM = pl.BlockSpec(memory_space=pltpu.SMEM)
HBM = pl.BlockSpec(memory_space=pl.ANY)


def norm_rows(x):
    values = x.astype(jnp.float32)
    scale = lax.rsqrt(jnp.mean(values * values, axis=-1, keepdims=True) + 1e-06)
    return (values * scale).astype(jnp.bfloat16)


def route_kernel(ids_ref, placing_ref, target_ref, *, experts, block_rows):
    replicas, rows, _ = ids_ref.shape
    share = rows // block_rows * CAP
    row = lax.broadcasted_iota(jnp.int32, (rows, rows), 0)
    col = lax.broadcasted_iota(jnp.int32, (rows, rows), 1)
    earlier = jnp.logical_and(col < row, col // block_rows == row // block_rows).astype(jnp.bfloat16)
    expert_range = lax.broadcasted_iota(jnp.int32, (rows, experts), 1)
    block_start = lax.broadcasted_iota(jnp.int32, (rows, 1), 0) // block_rows * CAP
    slot_range = lax.broadcasted_iota(jnp.int32, (rows, experts * share), 1)
    for r in range(replicas):
        ids = ids_ref[r]
        named = [(ids[:, k : k + 1] == expert_range).astype(jnp.float32) for k in range(2)]
        counts = jnp.dot(
            earlier, (named[0] + named[1]).astype(jnp.bfloat16), preferred_element_type=jnp.float32
        )
        targets = []
        for k in range(2):
            rank = jnp.sum(named[k] * counts, axis=-1, keepdims=True).astype(jnp.int32)
            targets.append(ids[:, k : k + 1] * share + block_start + rank)
        placed = jnp.logical_or(slot_range == targets[0], slot_range == targets[1])
        placing_ref[r] = placed.astype(jnp.float32).T.astype(jnp.bfloat16)
        target_ref[r] = jnp.concatenate(targets, axis=1)


def prepare_kernel(x_ref, placing_ref, out_ref):
    replicas = x_ref.shape[0]
    slots = placing_ref.shape[1]
    for r in range(replicas):
        normed = norm_rows(x_ref[r])
        out_ref[r * slots : (r + 1) * slots] = jnp.dot(
            placing_ref[r], normed, preferred_element_type=jnp.float32
        ).astype(jnp.bfloat16)


def gates_kernel(x_ref, router_ref, ids_ref, target_ref, mix_ref, *, slots):
    replicas, rows, _ = x_ref.shape
    experts = router_ref.shape[2]
    expert_range = lax.broadcasted_iota(jnp.int32, (rows, experts), 1)
    slot_range = lax.broadcasted_iota(jnp.int32, (rows, slots), 1)
    for r in range(replicas):
        normed = norm_rows(x_ref[r])
        logits = jnp.dot(
            normed.astype(jnp.float32),
            router_ref[r],
            precision=lax.Precision.HIGHEST,
            preferred_element_type=jnp.float32,
        )
        scores = 1.0 / (1.0 + jnp.exp(-logits))
        ids = ids_ref[r]
        picked = [
            jnp.sum(jnp.where(ids[:, k : k + 1] == expert_range, scores, 0.0), axis=-1, keepdims=True)
            for k in range(2)
        ]
        total = picked[0] + picked[1]
        target = target_ref[r]
        mix = sum(
            jnp.where(slot_range == target[:, k : k + 1], picked[k] / total, 0.0) for k in range(2)
        )
        high = mix.astype(jnp.bfloat16)
        mix_ref[r, :rows] = high
        mix_ref[r, rows:] = (mix - high.astype(jnp.float32)).astype(jnp.bfloat16)


def combine_kernel(section_ref, x_ref, mix_ref, answers_ref, kept_ref, out_ref, *, layer):
    replicas, rows, _ = x_ref.shape
    slots = mix_ref.shape[2]
    active = section_ref[0] == layer
    for r in range(replicas):
        both = jnp.dot(
            mix_ref[r], answers_ref[r * slots : (r + 1) * slots], preferred_element_type=jnp.float32
        )
        result = (x_ref[r].astype(jnp.float32) + (both[:rows] + both[rows:])).astype(jnp.bfloat16)
        out_ref[r] = jnp.where(active, result, kept_ref[r])


def expert_kernel(
    section_ref, rows_ref, gate_hbm, up_hbm, down_hbm, out_ref,
    gate_buf, up_buf, down_buf, inner_buf, sems, *, layer, chunk, out_chunk,
):
    width, hidden = gate_hbm.shape
    total = rows_ref.shape[0]
    row_step = min(total, 256)
    pieces = hidden // chunk
    out_pieces = width // out_chunk

    @pl.when(section_ref[0] == layer)
    def _():
        copies = []
        for j in range(pieces):
            part = pl.ds(j * chunk, chunk)
            first = pltpu.make_async_copy(gate_hbm.at[:, part], gate_buf.at[:, part], sems.at[0, j])
            second = pltpu.make_async_copy(up_hbm.at[:, part], up_buf.at[:, part], sems.at[1, j])
            first.start()
            second.start()
            copies.append((first, second))
        down_copies = []
        for j in range(out_pieces):
            part = pl.ds(j * out_chunk, out_chunk)
            copy = pltpu.make_async_copy(down_hbm.at[:, part], down_buf.at[:, part], sems.at[2, j])
            copy.start()
            down_copies.append(copy)
        for j in range(pieces):
            copies[j][0].wait()
            copies[j][1].wait()
            part = slice(j * chunk, (j + 1) * chunk)
            for i in range(0, total, row_step):
                block = rows_ref[i : i + row_step]
                gate_val = jnp.dot(block, gate_buf[:, part], preferred_element_type=jnp.float32)
                up_val = jnp.dot(block, up_buf[:, part], preferred_element_type=jnp.float32)
                act = gate_val / (1.0 + jnp.exp(-gate_val)) * up_val
                inner_buf[i : i + row_step, part] = act.astype(jnp.bfloat16)
        for j in range(out_pieces):
            down_copies[j].wait()
            part = slice(j * out_chunk, (j + 1) * out_chunk)
            for i in range(0, total, row_step):
                out_ref[i : i + row_step, part] = jnp.dot(
                    inner_buf[i : i + row_step], down_buf[:, part], preferred_element_type=jnp.float32
                ).astype(jnp.bfloat16)


def per_device(tokens, expert_ids, router_weight, w_gate, w_up, w_down):
    batches, replicas, tok_dev, width = tokens.shape
    experts = router_weight.shape[3]
    hidden = w_gate.shape[3]
    sections = lax.axis_size("section")
    section = lax.axis_index("section").astype(jnp.int32).reshape(1)
    rows = batches * tok_dev
    block_rows = tok_dev // 2
    share = rows // block_rows * CAP
    slots = experts * share
    gate_mat, up_mat, down_mat = w_gate[0, 0], w_up[0, 0], w_down[0, 0]
    router = router_weight[0]
    ids = jnp.swapaxes(expert_ids[0], 0, 1).reshape(replicas, rows, 2)
    chunk, out_chunk = 256, 256

    placing, target = pl.pallas_call(
        lambda *refs: route_kernel(*refs, experts=experts, block_rows=block_rows),
        out_shape=(
            jax.ShapeDtypeStruct((replicas, slots, rows), jnp.bfloat16),
            jax.ShapeDtypeStruct((replicas, rows, 2), jnp.int32),
        ),
        in_specs=[VMEM],
        out_specs=(VMEM, VMEM),
        name="route",
    )(ids)

    def prepare(x):
        return pl.pallas_call(
            prepare_kernel,
            out_shape=jax.ShapeDtypeStruct((replicas * slots, width), jnp.bfloat16),
            in_specs=[VMEM, VMEM],
            out_specs=VMEM,
            name="prepare",
        )(x, placing)

    def gates(x):
        return pl.pallas_call(
            lambda *refs: gates_kernel(*refs, slots=slots),
            out_shape=jax.ShapeDtypeStruct((replicas, 2 * rows, slots), jnp.bfloat16),
            in_specs=[VMEM] * 4,
            out_specs=VMEM,
            name="gates",
        )(x, router, ids, target)

    def expert(received, layer):
        total = received.shape[0]
        return pl.pallas_call(
            lambda *refs: expert_kernel(*refs, layer=layer, chunk=chunk, out_chunk=out_chunk),
            out_shape=jax.ShapeDtypeStruct((total, width), jnp.bfloat16),
            in_specs=[SMEM, VMEM, HBM, HBM, HBM],
            out_specs=VMEM,
            scratch_shapes=[
                pltpu.VMEM((width, hidden), jnp.bfloat16),
                pltpu.VMEM((width, hidden), jnp.bfloat16),
                pltpu.VMEM((hidden, width), jnp.bfloat16),
                pltpu.VMEM((total, hidden), jnp.bfloat16),
                pltpu.SemaphoreType.DMA((3, max(hidden // chunk, width // out_chunk))),
            ],
            compiler_params=pltpu.CompilerParams(vmem_limit_bytes=40 << 20),
            name="expert",
        )(section, received, gate_mat, up_mat, down_mat)

    def combine(x, mix, answers, kept, layer):
        return pl.pallas_call(
            lambda *refs: combine_kernel(*refs, layer=layer),
            out_shape=jax.ShapeDtypeStruct((replicas, rows, width), jnp.bfloat16),
            in_specs=[SMEM] + [VMEM] * 4,
            out_specs=VMEM,
            name="combine",
        )(section, x, mix, answers, kept)

    def exchange(array):
        return lax.all_to_all(array, "expert", split_axis=0, concat_axis=0, tiled=True)

    current = jnp.swapaxes(tokens, 0, 1).reshape(replicas, rows, width)
    kept = current
    for layer in range(sections):
        received = exchange(prepare(current))
        mix = gates(current)
        answers = exchange(expert(received, layer))
        kept = combine(current, mix, answers, kept, layer)
        if layer + 1 < sections:
            current = lax.ppermute(kept, "section", [(layer, layer + 1)])
    out = jnp.swapaxes(kept.reshape(replicas, batches, tok_dev, width), 0, 1)
    return out[None]


def solution(mesh):
    in_specs = (
        P(None, None, "expert", None),
        P("section", None, None, "expert", None),
        P("section", None, None, None),
        P("section", "expert", None, None),
        P("section", "expert", None, None),
        P("section", "expert", None, None),
    )
    out_specs = P("section", None, None, "expert", None)
    return jax.shard_map(
        per_device, mesh=mesh, in_specs=in_specs, out_specs=out_specs, check_vma=False
    )
```

time: 240 us -> 202 us (0.84)
  matrix products: 45 us -> 0 us
  blocking collectives: 0 us -> 39.3 us
  Pallas kernels: 0 us -> 38.2 us
  starting transfers between devices: 56.6 us -> 20.5 us
  waiting for transfers between devices: 101 us -> 70.1 us
  other arithmetic: 11.3 us -> 0 us
  local copies, waits for them, and re-layouts: 21.9 us -> 32 us
    dot_general x22 -> x0, matrix products: 45 us -> none  [the longest x4 21 us: working(): jnp.dot(inner, down_mat, preferred_element_type=jnp.float32)]
    all_to_all x0 -> x3, blocking collectives: none -> 39.3 us  [exchange(): lax.all_to_all(array, 'expert', split_axis=0, concat_axis=0, tiled=True)]
    pallas_call x0 -> x17, Pallas kernels: none -> 38.2 us  [the longest x4 10.7 us: expert(): pl.pallas_call(lambda *refs: expert_kernel(*refs, layer=layer, chunk=chun...]
    all_to_all x14 -> x5, waiting for transfers between devices: 68.4 us -> 38.2 us  [exchange(): lax.all_to_all(array, 'expert', split_axis=0, concat_axis=0, tiled=True)]
    unnamed x2 -> x41, local copies, waits for them, and re-layouts: 0.65 us -> 30.6 us
    all_to_all x14 -> x5, starting transfers between devices: 47.6 us -> 17.7 us  [exchange(): lax.all_to_all(array, 'expert', split_axis=0, concat_axis=0, tiled=True)]
    reduce_sum x35 -> x0, other arithmetic: 9.94 us -> none  [the longest x7 6.18 us: prepare(): jnp.mean(values * values, axis=-1, keepdims=True) + 1e-06]
    ppermute x7 -> x3, starting transfers between devices: 9.04 us -> 2.77 us  [per_device(): current = lax.ppermute(kept, 'section', [(layer, layer + 1)])]
  transfers between devices with their start and end apart: 21 -> 8, of which waited for: 21 -> 6; matrix products, arithmetic and copies ran while one was open for 10% -> 0% of each run, Pallas kernels for 0% -> 5%
where the time goes in v1:
time: 202 us; the launch traced here: 200 us
  waiting for transfers between devices  70.1 us (35%)
  blocking collectives  39.3 us (19%)
  Pallas kernels  38.2 us (19%)
  local copies, waits for them, and re-layouts  32 us (16%)
  starting transfers between devices  20.5 us (10%)
    all_to_all x3, blocking collectives, exchange(): lax.all_to_all(array, 'expert', split_axis=0, concat_axis=0, tiled=True)  39.3 us
    all_to_all x5, waiting for transfers between devices, exchange(): lax.all_to_all(array, 'expert', split_axis=0, concat_axis=0, tiled=True)  38.2 us
    ppermute x3, waiting for transfers between devices, per_device(): current = lax.ppermute(kept, 'section', [(layer, layer + 1)])  31.9 us
    unnamed x41, local copies, waits for them, and re-layouts  30.6 us
    all_to_all x5, starting transfers between devices, exchange(): lax.all_to_all(array, 'expert', split_axis=0, concat_axis=0, tiled=True)  17.7 us
    pallas_call x4, Pallas kernels, expert(): pl.pallas_call(lambda *refs: expert_kernel(*refs, layer=layer, chunk=chun...  10.7 us
    pallas_call x4, Pallas kernels, gates(): pl.pallas_call(lambda *refs: gates_kernel(*refs, slots=slots), out_shape=...  9.09 us
    pallas_call x4, Pallas kernels, prepare(): pl.pallas_call(prepare_kernel, out_shape=jax.ShapeDtypeStruct((replicas *...  8.34 us
  transfers between devices with their start and end apart: 8, of which 6 were waited for; matrix products, arithmetic and copies ran while one was open for 0% of the time, Pallas kernels for 5%

profile of v1, /device:TPU:24, one launch (start us, length us, event | category | flops | bytes accessed | tf_op | source)
XLA Modules:
  0.0 200.3 jit_solution(12569224279222988585)
XLA Ops:
  3.2 2.1 %prepare.4 = bf16[256,1024]{1,0:T(8,128)(2,1)} custom-call(bf16[1,64,1024]{2,1,0:T(8,128)(2,1)} %bitcast.54, bf16[1,256,64]{2,1,0:T(8,128)(2,1)} %get-tuple-element.8.placing_ref), custom_call_target="tpu_custom_call" | custom-call | tf_op jit(solution)/shard_map/prepare/pallas_call | solution.py:167
  5.3 3.7 %all-to-all-start = ((bf16[8,32,1024]{2,1,0:T(8,128)(2,1)}), bf16[8,32,1024]{2,1,0:T(8,128)(2,1)S(1)}, u32[]{:S(2)}, u32[]{:S(2)}) async-start(bf16[8,32,1024]{2,1,0:T(8,128)(2,1)} %bitcast.50), calls=%async_computation | async-start | bytes 1048576 | tf_op jit(solution)/shard_map/all_to_all | solution.py:212
  9.0 9.7 %all-to-all-done = bf16[8,32,1024]{2,1,0:T(8,128)(2,1)S(1)} async-done(((bf16[8,32,1024]{2,1,0:T(8,128)(2,1)}), bf16[8,32,1024]{2,1,0:T(8,128)(2,1)S(1)}, u32[]{:S(2)}, u32[]{:S(2)}) %all-to-all-start) | async-done | bytes 524320 | tf_op jit(solution)/shard_map/all_to_all | solution.py:212
  25.9 3.5 %all-to-all-start.1 = ((bf16[8,32,1024]{2,1,0:T(8,128)(2,1)}), bf16[8,32,1024]{2,1,0:T(8,128)(2,1)S(1)}, u32[]{:S(2)}, u32[]{:S(2)}) async-start(bf16[8,32,1024]{2,1,0:T(8,128)(2,1)} %bitcast.9), calls=%async_computation.1 | async-start | bytes 1048576 | tf_op jit(solution)/shard_map/all_to_all | solution.py:212
  30.4 2.3 %gates.4.refs_2_ = bf16[1,128,256]{2,1,0:T(8,128)(2,1)} custom-call(bf16[1,64,1024]{2,1,0:T(8,128)(2,1)} %bitcast.55, f32[1,1024,8]{2,1,0:T(8,128)} %bitcast.42, s32[1,64,2]{2,1,0:T(8,128)} %bitcast.59, s32[1,64,2]{2,1,0:T(8,128)} %get-tuple-element.7.refs_3_), custom_call_target="tpu_custom_call" | custom-call | tf_op jit(solution)/shard_map/gates/pallas_call | solution.py:176
  32.7 6.4 %all-to-all-done.1 = bf16[8,32,1024]{2,1,0:T(8,128)(2,1)S(1)} async-done(((bf16[8,32,1024]{2,1,0:T(8,128)(2,1)}), bf16[8,32,1024]{2,1,0:T(8,128)(2,1)S(1)}, u32[]{:S(2)}, u32[]{:S(2)}) %all-to-all-start.1) | async-done | bytes 524320 | tf_op jit(solution)/shard_map/all_to_all | solution.py:212
  43.2 2.1 %prepare.5 = bf16[256,1024]{1,0:T(8,128)(2,1)} custom-call(bf16[1,64,1024]{2,1,0:T(8,128)(2,1)} %copy-done.17, bf16[1,256,64]{2,1,0:T(8,128)(2,1)} %get-tuple-element.8.placing_ref), custom_call_target="tpu_custom_call" | custom-call | tf_op jit(solution)/shard_map/prepare/pallas_call | solution.py:167
  45.3 13.1 %all_to_all.88 = bf16[8,32,1024]{2,1,0:T(8,128)(2,1)S(1)} all-to-all(bf16[8,32,1024]{2,1,0:T(8,128)(2,1)} %bitcast.52), channel_id=1, replica_groups=mesh['section'=4,'expert'=8] {'expert'}, dimensions={0} | all-to-all | bytes 1048576 | tf_op jit(solution)/shard_map/all_to_all | solution.py:212
  65.5 3.5 %all-to-all-start.3 = ((bf16[8,32,1024]{2,1,0:T(8,128)(2,1)}), bf16[8,32,1024]{2,1,0:T(8,128)(2,1)S(1)}, u32[]{:S(2)}, u32[]{:S(2)}) async-start(bf16[8,32,1024]{2,1,0:T(8,128)(2,1)} %bitcast.13), calls=%async_computation.3 | async-start | bytes 1048576 | tf_op jit(solution)/shard_map/all_to_all | solution.py:212
  69.1 2.3 %gates.5.refs_2_ = bf16[1,128,256]{2,1,0:T(8,128)(2,1)} custom-call(bf16[1,64,1024]{2,1,0:T(8,128)(2,1)} %copy-done.17, f32[1,1024,8]{2,1,0:T(8,128)} %bitcast.43, s32[1,64,2]{2,1,0:T(8,128)} %bitcast.60, s32[1,64,2]{2,1,0:T(8,128)} %get-tuple-element.7.refs_3_), custom_call_target="tpu_custom_call" | custom-call | tf_op jit(solution)/shard_map/gates/pallas_call | solution.py:176
  71.3 7.4 %all-to-all-done.3 = bf16[8,32,1024]{2,1,0:T(8,128)(2,1)S(1)} async-done(((bf16[8,32,1024]{2,1,0:T(8,128)(2,1)}), bf16[8,32,1024]{2,1,0:T(8,128)(2,1)S(1)}, u32[]{:S(2)}, u32[]{:S(2)}) %all-to-all-start.3) | async-done | bytes 524320 | tf_op jit(solution)/shard_map/all_to_all | solution.py:212
  79.5 2.1 %combine.5.refs_4_ = bf16[1,64,1024]{2,1,0:T(8,128)(2,1)} custom-call(s32[1]{0:T(128)} %bitcast.refs_0_, bf16[1,64,1024]{2,1,0:T(8,128)(2,1)} %copy-done.17, bf16[1,128,256]{2,1,0:T(8,128)(2,1)} %gates.5.refs_2_, bf16[256,1024]{1,0:T(8,128)(2,1)} %bitcast.48, bf16[1,64,1024]{2,1,0:T(8,128)(2,1)} %combine.4.refs_4_), custom_call_target="tpu_custom_call" | custom-call | tf_op jit(solution)/shard_map/combine/pallas_call | solution.py:203
  83.1 2.1 %prepare.6 = bf16[256,1024]{1,0:T(8,128)(2,1)} custom-call(bf16[1,64,1024]{2,1,0:T(8,128)(2,1)} %copy-done.18, bf16[1,256,64]{2,1,0:T(8,128)(2,1)} %get-tuple-element.8.placing_ref), custom_call_target="tpu_custom_call" | custom-call | tf_op jit(solution)/shard_map/prepare/pallas_call | solution.py:167
  85.2 13.1 %all_to_all.89 = bf16[8,32,1024]{2,1,0:T(8,128)(2,1)S(1)} all-to-all(bf16[8,32,1024]{2,1,0:T(8,128)(2,1)} %bitcast.53), channel_id=1, replica_groups=mesh['section'=4,'expert'=8] {'expert'}, dimensions={0} | all-to-all | bytes 1048576 | tf_op jit(solution)/shard_map/all_to_all | solution.py:212
  105.4 3.5 %all-to-all-start.5 = ((bf16[8,32,1024]{2,1,0:T(8,128)(2,1)}), bf16[8,32,1024]{2,1,0:T(8,128)(2,1)S(1)}, u32[]{:S(2)}, u32[]{:S(2)}) async-start(bf16[8,32,1024]{2,1,0:T(8,128)(2,1)} %bitcast.17), calls=%async_computation.5 | async-start | bytes 1048576 | tf_op jit(solution)/shard_map/all_to_all | solution.py:212
  108.9 2.3 %gates.6.refs_2_ = bf16[1,128,256]{2,1,0:T(8,128)(2,1)} custom-call(bf16[1,64,1024]{2,1,0:T(8,128)(2,1)} %copy-done.18, f32[1,1024,8]{2,1,0:T(8,128)} %bitcast.44, s32[1,64,2]{2,1,0:T(8,128)} %bitcast.61, s32[1,64,2]{2,1,0:T(8,128)} %get-tuple-element.7.refs_3_), custom_call_target="tpu_custom_call" | custom-call | tf_op jit(solution)/shard_map/gates/pallas_call | solution.py:176
  111.2 7.4 %all-to-all-done.5 = bf16[8,32,1024]{2,1,0:T(8,128)(2,1)S(1)} async-done(((bf16[8,32,1024]{2,1,0:T(8,128)(2,1)}), bf16[8,32,1024]{2,1,0:T(8,128)(2,1)S(1)}, u32[]{:S(2)}, u32[]{:S(2)}) %all-to-all-start.5) | async-done | bytes 524320 | tf_op jit(solution)/shard_map/all_to_all | solution.py:212
  122.7 31.9 %collective-permute-done.2.refs_0_.x_ref.refs_1_ = bf16[1,64,1024]{2,1,0:T(8,128)(2,1)S(1)} collective-permute-done((bf16[1,64,1024]{2,1,0:T(8,128)(2,1)}, bf16[1,64,1024]{2,1,0:T(8,128)(2,1)S(1)}, u32[]{:S(2)}, u32[]{:S(2)}) %collective-permute-start.2) | collective-permute-done | bytes 131104 | tf_op jit(solution)/shard_map/ppermute | solution.py:222
  155.2 2.1 %prepare.7 = bf16[256,1024]{1,0:T(8,128)(2,1)} custom-call(bf16[1,64,1024]{2,1,0:T(8,128)(2,1)} %copy-done.16, bf16[1,256,64]{2,1,0:T(8,128)(2,1)} %get-tuple-element.8.placing_ref), custom_call_target="tpu_custom_call" | custom-call | tf_op jit(solution)/shard_map/prepare/pallas_call | solution.py:167
  157.3 13.1 %all_to_all.90 = bf16[8,32,1024]{2,1,0:T(8,128)(2,1)S(1)} all-to-all(bf16[8,32,1024]{2,1,0:T(8,128)(2,1)} %bitcast.51), channel_id=1, replica_groups=mesh['section'=4,'expert'=8] {'expert'}, dimensions={0} | all-to-all | bytes 1048576 | tf_op jit(solution)/shard_map/all_to_all | solution.py:212
  176.6 7.7 %expert.7 = bf16[256,1024]{1,0:T(8,128)(2,1)} custom-call(s32[1]{0:T(128)} %bitcast.refs_0_, bf16[256,1024]{1,0:T(8,128)(2,1)S(1)} %bitcast.41, bf16[1024,1792]{1,0:T(8,128)(2,1)S(1)} %bitcast.29, bf16[1024,1792]{1,0:T(8,128)(2,1)S(1)} %bitcast.33, bf16[1792,1024]{1,0:T(8,128)(2,1)S(1)} %bitcast.37), custom_call_target="tpu_custom_call" | custom-call | tf_op jit(solution)/shard_map/expert/pallas_call | solution.py:186
  184.3 3.5 %all-to-all-start.7 = ((bf16[8,32,1024]{2,1,0:T(8,128)(2,1)}), bf16[8,32,1024]{2,1,0:T(8,128)(2,1)S(1)}, u32[]{:S(2)}, u32[]{:S(2)}) async-start(bf16[8,32,1024]{2,1,0:T(8,128)(2,1)} %bitcast.21), calls=%async_computation.7 | async-start | bytes 1048576 | tf_op jit(solution)/shard_map/all_to_all | solution.py:212
  187.8 2.3 %gates.7.refs_2_ = bf16[1,128,256]{2,1,0:T(8,128)(2,1)} custom-call(bf16[1,64,1024]{2,1,0:T(8,128)(2,1)} %copy-done.16, f32[1,1024,8]{2,1,0:T(8,128)} %bitcast.45, s32[1,64,2]{2,1,0:T(8,128)} %bitcast.62, s32[1,64,2]{2,1,0:T(8,128)} %get-tuple-element.7.refs_3_), custom_call_target="tpu_custom_call" | custom-call | tf_op jit(solution)/shard_map/gates/pallas_call | solution.py:176
  190.0 7.4 %all-to-all-done.7 = bf16[8,32,1024]{2,1,0:T(8,128)(2,1)S(1)} async-done(((bf16[8,32,1024]{2,1,0:T(8,128)(2,1)}), bf16[8,32,1024]{2,1,0:T(8,128)(2,1)S(1)}, u32[]{:S(2)}, u32[]{:S(2)}) %all-to-all-start.7) | async-done | bytes 524320 | tf_op jit(solution)/shard_map/all_to_all | solution.py:212
  (54 shorter events, 45.8 us)
Async XLA Ops:
  5.3 13.4 %all-to-all-start = ((bf16[8,32,1024]{2,1,0:T(8,128)(2,1)}), bf16[8,32,1024]{2,1,0:T(8,128)(2,1)S(1)}, u32[]{:S(2)}, u32[]{:S(2)}) async-start(bf16[8,32,1024]{2,1,0:T(8,128)(2,1)} %bitcast.50), calls=%async_computation | async-start | bytes 1048576 | tf_op jit(solution)/shard_map/all_to_all | solution.py:212
  18.7 2.0 %copy-start = (bf16[1,1,1024,1792]{3,2,1,0:T(8,128)(2,1)S(1)}, bf16[1,1,1024,1792]{3,2,1,0:T(8,128)(2,1)}, u32[]{:S(2)}) copy-start(bf16[1,1,1024,1792]{3,2,1,0:T(8,128)(2,1)} %param.9) | copy-start | bytes 11010052
  20.8 2.0 %copy-start.4 = (bf16[1,1,1024,1792]{3,2,1,0:T(8,128)(2,1)S(1)}, bf16[1,1,1024,1792]{3,2,1,0:T(8,128)(2,1)}, u32[]{:S(2)}) copy-start(bf16[1,1,1024,1792]{3,2,1,0:T(8,128)(2,1)} %param.10) | copy-start | bytes 11010052
  22.8 2.0 %copy-start.8 = (bf16[1,1,1792,1024]{3,2,1,0:T(8,128)(2,1)S(1)}, bf16[1,1,1792,1024]{3,2,1,0:T(8,128)(2,1)}, u32[]{:S(2)}) copy-start(bf16[1,1,1792,1024]{3,2,1,0:T(8,128)(2,1)} %param.11) | copy-start | bytes 11010052
  24.9 4.5 %copy-start.19 = (f32[1,1,1024,8]{2,3,1,0:T(8,128)S(1)}, f32[1,1,1024,8]{2,3,1,0:T(8,128)}, u32[]{:S(2)}) copy-start(f32[1,1,1024,8]{2,3,1,0:T(8,128)} %param.8) | copy-start | bytes 98308
  25.9 13.2 %all-to-all-start.1 = ((bf16[8,32,1024]{2,1,0:T(8,128)(2,1)}), bf16[8,32,1024]{2,1,0:T(8,128)(2,1)S(1)}, u32[]{:S(2)}, u32[]{:S(2)}) async-start(bf16[8,32,1024]{2,1,0:T(8,128)(2,1)} %bitcast.9), calls=%async_computation.1 | async-start | bytes 1048576 | tf_op jit(solution)/shard_map/all_to_all | solution.py:212
  39.0 0.8 copy-start.13
  41.9 0.7 collective-permute-start
  58.4 2.0 %copy-start.1 = (bf16[1,1,1024,1792]{3,2,1,0:T(8,128)(2,1)S(1)}, bf16[1,1,1024,1792]{3,2,1,0:T(8,128)(2,1)}, u32[]{:S(2)}) copy-start(bf16[1,1,1024,1792]{3,2,1,0:T(8,128)(2,1)} %param.9) | copy-start | bytes 11010052
  60.5 2.0 %copy-start.5 = (bf16[1,1,1024,1792]{3,2,1,0:T(8,128)(2,1)S(1)}, bf16[1,1,1024,1792]{3,2,1,0:T(8,128)(2,1)}, u32[]{:S(2)}) copy-start(bf16[1,1,1024,1792]{3,2,1,0:T(8,128)(2,1)} %param.10) | copy-start | bytes 11010052
  62.5 2.0 %copy-start.9 = (bf16[1,1,1792,1024]{3,2,1,0:T(8,128)(2,1)S(1)}, bf16[1,1,1792,1024]{3,2,1,0:T(8,128)(2,1)}, u32[]{:S(2)}) copy-start(bf16[1,1,1792,1024]{3,2,1,0:T(8,128)(2,1)} %param.11) | copy-start | bytes 11010052
  65.5 13.2 %all-to-all-start.3 = ((bf16[8,32,1024]{2,1,0:T(8,128)(2,1)}), bf16[8,32,1024]{2,1,0:T(8,128)(2,1)S(1)}, u32[]{:S(2)}, u32[]{:S(2)}) async-start(bf16[8,32,1024]{2,1,0:T(8,128)(2,1)} %bitcast.13), calls=%async_computation.3 | async-start | bytes 1048576 | tf_op jit(solution)/shard_map/all_to_all | solution.py:212
  78.7 0.8 copy-start.14
  81.6 0.8 collective-permute-start.1
  98.3 2.0 %copy-start.2 = (bf16[1,1,1024,1792]{3,2,1,0:T(8,128)(2,1)S(1)}, bf16[1,1,1024,1792]{3,2,1,0:T(8,128)(2,1)}, u32[]{:S(2)}) copy-start(bf16[1,1,1024,1792]{3,2,1,0:T(8,128)(2,1)} %param.9) | copy-start | bytes 11010052
  100.3 2.0 %copy-start.6 = (bf16[1,1,1024,1792]{3,2,1,0:T(8,128)(2,1)S(1)}, bf16[1,1,1024,1792]{3,2,1,0:T(8,128)(2,1)}, u32[]{:S(2)}) copy-start(bf16[1,1,1024,1792]{3,2,1,0:T(8,128)(2,1)} %param.10) | copy-start | bytes 11010052
  102.4 2.0 %copy-start.10 = (bf16[1,1,1792,1024]{3,2,1,0:T(8,128)(2,1)S(1)}, bf16[1,1,1792,1024]{3,2,1,0:T(8,128)(2,1)}, u32[]{:S(2)}) copy-start(bf16[1,1,1792,1024]{3,2,1,0:T(8,128)(2,1)} %param.11) | copy-start | bytes 11010052
  105.4 13.2 %all-to-all-start.5 = ((bf16[8,32,1024]{2,1,0:T(8,128)(2,1)}), bf16[8,32,1024]{2,1,0:T(8,128)(2,1)S(1)}, u32[]{:S(2)}, u32[]{:S(2)}) async-start(bf16[8,32,1024]{2,1,0:T(8,128)(2,1)} %bitcast.17), calls=%async_computation.5 | async-start | bytes 1048576 | tf_op jit(solution)/shard_map/all_to_all | solution.py:212
  118.6 0.8 copy-start.15
  121.4 33.2 %collective-permute-start.2 = (bf16[1,64,1024]{2,1,0:T(8,128)(2,1)}, bf16[1,64,1024]{2,1,0:T(8,128)(2,1)S(1)}, u32[]{:S(2)}, u32[]{:S(2)}) collective-permute-start(bf16[1,64,1024]{2,1,0:T(8,128)(2,1)} %combine.6.refs_4_), channel_id=1, source_target_pairs={{16,24},{17,25},{18,26},{19,27},{20,28},{21,29},{22,30},{23,31}} | collective-permute-start | bytes 393224 | tf_op jit(solution)/shard_map/ppermute | solution.py:222
  170.4 2.0 %copy-start.3 = (bf16[1,1,1024,1792]{3,2,1,0:T(8,128)(2,1)S(1)}, bf16[1,1,1024,1792]{3,2,1,0:T(8,128)(2,1)}, u32[]{:S(2)}) copy-start(bf16[1,1,1024,1792]{3,2,1,0:T(8,128)(2,1)} %param.9) | copy-start | bytes 11010052
  172.5 2.0 %copy-start.7 = (bf16[1,1,1024,1792]{3,2,1,0:T(8,128)(2,1)S(1)}, bf16[1,1,1024,1792]{3,2,1,0:T(8,128)(2,1)}, u32[]{:S(2)}) copy-start(bf16[1,1,1024,1792]{3,2,1,0:T(8,128)(2,1)} %param.10) | copy-start | bytes 11010052
  174.5 2.0 %copy-start.11 = (bf16[1,1,1792,1024]{3,2,1,0:T(8,128)(2,1)S(1)}, bf16[1,1,1792,1024]{3,2,1,0:T(8,128)(2,1)}, u32[]{:S(2)}) copy-start(bf16[1,1,1792,1024]{3,2,1,0:T(8,128)(2,1)} %param.11) | copy-start | bytes 11010052
  184.3 13.2 %all-to-all-start.7 = ((bf16[8,32,1024]{2,1,0:T(8,128)(2,1)}), bf16[8,32,1024]{2,1,0:T(8,128)(2,1)S(1)}, u32[]{:S(2)}, u32[]{:S(2)}) async-start(bf16[8,32,1024]{2,1,0:T(8,128)(2,1)} %bitcast.21), calls=%async_computation.7 | async-start | bytes 1048576 | tf_op jit(solution)/shard_map/all_to_all | solution.py:212
  (4 other events, 2.8 us)

commit v2 on v0

v2 whole, which is shorter than its diff:
```python
import jax
import jax.numpy as jnp
from jax import lax
from jax.experimental import pallas as pl
from jax.experimental.pallas import tpu as pltpu
from jax.sharding import PartitionSpec as P

CAP = 4
CHUNK = 256
UNITS = 1
VMEM = pl.BlockSpec(memory_space=pltpu.VMEM)
SMEM = pl.BlockSpec(memory_space=pltpu.SMEM)


def near(array):
    return pltpu.with_memory_space_constraint(array, pltpu.VMEM)


def norm_rows(x):
    values = x.astype(jnp.float32)
    scale = lax.rsqrt(jnp.mean(values * values, axis=-1, keepdims=True) + 1e-06)
    return (values * scale).astype(jnp.bfloat16)


def unit_of(section_ref, step, units):
    return jnp.clip(step - section_ref[0], 0, units - 1)


def is_active(section_ref, step, units):
    return jnp.logical_and(step >= section_ref[0], step - section_ref[0] < units)


def start_kernel(
    section_ref, ids_ref, tokens_ref, placing_ref, target_ref, x_ref, out_ref, *, experts, units
):
    _, batches, replicas, _, tok_dev = ids_ref.shape
    span = batches // units
    rows = span * tok_dev
    block_rows = tok_dev // 2
    share = rows // block_rows * CAP
    slots = experts * share
    row = lax.broadcasted_iota(jnp.int32, (rows, rows), 0)
    col = lax.broadcasted_iota(jnp.int32, (rows, rows), 1)
    earlier = jnp.logical_and(row < col, row // block_rows == col // block_rows)
    earlier = earlier.astype(jnp.float32).astype(jnp.bfloat16)
    expert_range = lax.broadcasted_iota(jnp.int32, (experts, rows), 0)
    block_start = lax.broadcasted_iota(jnp.int32, (1, rows), 1) // block_rows * CAP
    slot_range = lax.broadcasted_iota(jnp.int32, (slots, rows), 0)
    for u in range(units):
        for r in range(replicas):
            members = range(u * span, (u + 1) * span)
            ids = jnp.concatenate([ids_ref[0, m, r] for m in members], axis=1)
            named = [(ids[k : k + 1] == expert_range).astype(jnp.float32) for k in range(2)]
            counts = jnp.dot(
                (named[0] + named[1]).astype(jnp.bfloat16), earlier, preferred_element_type=jnp.float32
            )
            targets = []
            for k in range(2):
                rank = jnp.sum(named[k] * counts, axis=0, keepdims=True).astype(jnp.int32)
                targets.append(ids[k : k + 1] * share + block_start + rank)
                target_ref[u, r, k : k + 1] = targets[k]
            placed = jnp.logical_or(slot_range == targets[0], slot_range == targets[1])
            placing = placed.astype(jnp.float32).astype(jnp.bfloat16)
            placing_ref[u, r] = placing
            x = jnp.concatenate([tokens_ref[m, r] for m in members], axis=0)
            x_ref[u, r] = x
            if u == 0:
                out_ref[r * slots : (r + 1) * slots] = jnp.dot(
                    placing, norm_rows(x), preferred_element_type=jnp.float32
                ).astype(jnp.bfloat16)


def prepare_kernel(section_ref, incoming_ref, tokens_ref, placing_ref, x_ref, out_ref, *, step):
    units, replicas, slots, _ = placing_ref.shape
    unit = unit_of(section_ref, step, units)
    for r in range(replicas):
        x = incoming_ref[r]
        if step < units:
            x = jnp.where(section_ref[0] == 0, tokens_ref[unit, r], x)
        x_ref[r] = x
        out_ref[r * slots : (r + 1) * slots] = jnp.dot(
            placing_ref[unit, r], norm_rows(x), preferred_element_type=jnp.float32
        ).astype(jnp.bfloat16)


def mix_rows(x, router, ids, targets, slots):
    rows = x.shape[0]
    experts = router.shape[0]
    expert_range = lax.broadcasted_iota(jnp.int32, (experts, rows), 0)
    slot_range = lax.broadcasted_iota(jnp.int32, (slots, rows), 0)
    logits = lax.dot_general(
        router,
        norm_rows(x).astype(jnp.float32),
        (((1,), (1,)), ((), ())),
        precision=lax.Precision.HIGHEST,
        preferred_element_type=jnp.float32,
    )
    scores = 1.0 / (1.0 + jnp.exp(-logits))
    picked = [
        jnp.sum(jnp.where(ids[k : k + 1] == expert_range, scores, 0.0), axis=0, keepdims=True)
        for k in range(2)
    ]
    total = picked[0] + picked[1]
    return sum(
        jnp.where(slot_range == targets[k : k + 1], picked[k] / total, 0.0) for k in range(2)
    ).T


def expert_kernel(
    section_ref, rows_ref, gate_ref, up_ref, down_ref, x_ref, router_ref, ids_ref, target_ref,
    out_ref, mix_ref, inner_ref, *, step,
):
    width, hidden = gate_ref.shape
    total = rows_ref.shape[0]
    row_step = min(total, 256)
    units, replicas, _, _ = target_ref.shape
    span = ids_ref.shape[1] // units
    rows = x_ref.shape[1]
    slots = mix_ref.shape[2]
    unit = unit_of(section_ref, step, units)

    def run_rows(start):
        block = rows_ref[pl.ds(start, row_step)]
        for j in range(0, hidden, CHUNK):
            part = slice(j, j + CHUNK)
            gate_val = jnp.dot(block, gate_ref[:, part], preferred_element_type=jnp.float32)
            up_val = jnp.dot(block, up_ref[:, part], preferred_element_type=jnp.float32)
            inner_ref[:, part] = (gate_val / (1.0 + jnp.exp(-gate_val)) * up_val).astype(jnp.bfloat16)
        for j in range(0, width, CHUNK):
            part = slice(j, j + CHUNK)
            out_ref[pl.ds(start, row_step), part] = jnp.dot(
                inner_ref[...], down_ref[:, part], preferred_element_type=jnp.float32
            ).astype(jnp.bfloat16)

    @pl.when(is_active(section_ref, step, units))
    def _():
        for r in range(replicas):
            ids = jnp.concatenate([ids_ref[0, unit * span + m, r] for m in range(span)], axis=1)
            mix = mix_rows(x_ref[r], router_ref[0, r], ids, target_ref[unit, r], slots)
            high = mix.astype(jnp.bfloat16)
            mix_ref[r, :rows] = high
            mix_ref[r, rows:] = (mix - high.astype(jnp.float32)).astype(jnp.bfloat16)
        if total == row_step:
            run_rows(0)
        else:

            @pl.loop(0, total // row_step)
            def _(i):
                run_rows(pl.multiple_of(i * row_step, row_step))


def combine_kernel(section_ref, x_ref, mix_ref, answers_ref, kept_ref, out_ref, *refs, step, last):
    replicas, rows, _ = x_ref.shape
    units = kept_ref.shape[0]
    slots = mix_ref.shape[2]
    unit = unit_of(section_ref, step, units)
    active = is_active(section_ref, step, units)
    for r in range(replicas):
        both = jnp.dot(
            mix_ref[r], answers_ref[r * slots : (r + 1) * slots], preferred_element_type=jnp.float32
        )
        result = (x_ref[r].astype(jnp.float32) + (both[:rows] + both[rows:])).astype(jnp.bfloat16)
        for u in range(units):
            here = jnp.logical_and(active, unit == u)
            out_ref[u, r] = jnp.where(here, result, kept_ref[u, r])
        if not last:
            refs[0][r] = result


def per_device(tokens, expert_ids, router_weight, w_gate, w_up, w_down):
    batches, replicas, tok_dev, width = tokens.shape
    experts = router_weight.shape[3]
    hidden = w_gate.shape[3]
    sections = lax.axis_size("section")
    section = lax.axis_index("section").astype(jnp.int32).reshape(1)
    units = UNITS
    rows = batches // units * tok_dev
    slots = experts * (rows // (tok_dev // 2) * CAP)
    router = jnp.swapaxes(router_weight, 2, 3)
    ids = jnp.swapaxes(expert_ids, 3, 4)
    mats = tuple(w[0, 0] for w in (w_gate, w_up, w_down))
    params = pltpu.CompilerParams(vmem_limit_bytes=16 << 20)

    def call(kernel, name, args, shapes, scratch=(), **static):
        outs = tuple(
            jax.ShapeDtypeStruct(s.shape, s.dtype) if far else pltpu.VMEM(s.shape, s.dtype)
            for s, far in shapes
        )
        return pl.pallas_call(
            lambda *refs: kernel(*refs, **static),
            out_shape=outs,
            in_specs=[SMEM if a is section else VMEM for a in args],
            out_specs=(VMEM,) * len(outs),
            scratch_shapes=scratch,
            compiler_params=params,
            cost_estimate=pl.CostEstimate(flops=10**10, bytes_accessed=10**8, transcendentals=0),
            name=name,
        )(*(a if a is section or name == "start" else near(a) for a in args))

    def shape(*dims, dtype=jnp.bfloat16, far=False):
        return (jax.ShapeDtypeStruct(dims, dtype), far)

    def exchange(array):
        return lax.all_to_all(array, "expert", split_axis=0, concat_axis=0, tiled=True)

    placing, target, staged, outgoing = call(
        start_kernel,
        "start",
        (section, ids, tokens),
        (
            shape(units, replicas, slots, rows),
            shape(units, replicas, 2, rows, dtype=jnp.int32),
            shape(units, replicas, rows, width),
            shape(replicas * slots, width),
        ),
        experts=experts,
        units=units,
    )
    current, kept = staged[0], staged
    steps = sections + units - 1
    for step in range(steps):
        last = step + 1 == steps
        received = exchange(outgoing)
        total = received.shape[0]
        answers, mix = call(
            expert_kernel,
            "expert",
            (section, received, *mats, current, router, ids, target),
            (shape(total, width), shape(replicas, 2 * rows, slots)),
            scratch=[pltpu.VMEM((min(total, 256), hidden), jnp.bfloat16)],
            step=step,
        )
        outs = [shape(units, replicas, rows, width, far=last)]
        if not last:
            outs.append(shape(replicas, rows, width))
        kept, *result = call(
            combine_kernel,
            "combine",
            (section, current, mix, exchange(answers), kept),
            outs,
            step=step,
            last=last,
        )
        if not last:
            pairs = [(s, s + 1) for s in range(sections - 1) if 0 <= step - s < units]
            incoming = lax.ppermute(result[0], "section", pairs)
            current, outgoing = call(
                prepare_kernel,
                "prepare",
                (section, incoming, staged, placing),
                (shape(replicas, rows, width), shape(replicas * slots, width)),
                step=step + 1,
            )
    out = jnp.transpose(
        kept.reshape(units, replicas, batches // units, tok_dev, width), (0, 2, 1, 3, 4)
    )
    return out.reshape(1, batches, replicas, tok_dev, width)


def solution(mesh):
    in_specs = (
        P(None, None, "expert", None),
        P("section", None, None, "expert", None),
        P("section", None, None, None),
        P("section", "expert", None, None),
        P("section", "expert", None, None),
        P("section", "expert", None, None),
    )
    out_specs = P("section", None, None, "expert", None)
    return jax.shard_map(
        per_device, mesh=mesh, in_specs=in_specs, out_specs=out_specs, check_vma=False
    )
```

time: 240 us -> 132 us (0.55)
  blocking collectives: 0 us -> 98.4 us
  waiting for transfers between devices: 101 us -> 21.7 us
  starting transfers between devices: 56.6 us -> 2.63 us
  matrix products: 45 us -> 0 us
  local copies, waits for them, and re-layouts: 21.9 us -> 1.61 us
  other arithmetic: 11.3 us -> 0 us
  Pallas kernels: 0 us -> 6.66 us
    all_to_all x0 -> x8, blocking collectives: none -> 98.4 us  [exchange(): lax.all_to_all(array, 'expert', split_axis=0, concat_axis=0, tiled=True)]
    all_to_all x14 -> x0, waiting for transfers between devices: 68.4 us -> none  [the longest x7 37.4 us: serve(): lax.all_to_all(results, 'expert', split_axis=0, concat_axis=0, tiled=True)]
    all_to_all x14 -> x0, starting transfers between devices: 47.6 us -> none  [the longest x7 24 us: send_out(): lax.all_to_all(outgoing, 'expert', split_axis=0, concat_axis=0, tiled=True)]
    dot_general x22 -> x0, matrix products: 45 us -> none  [the longest x4 21 us: working(): jnp.dot(inner, down_mat, preferred_element_type=jnp.float32)]
    ppermute x7 -> x3, waiting for transfers between devices: 32.4 us -> 21.7 us  [per_device(): incoming = lax.ppermute(result[0], 'section', pairs)]
    reduce_sum x35 -> x0, other arithmetic: 9.94 us -> none  [the longest x7 6.18 us: prepare(): jnp.mean(values * values, axis=-1, keepdims=True) + 1e-06]
    pallas_call x0 -> x12, Pallas kernels: none -> 6.66 us  [call(): pl.pallas_call(lambda *refs: kernel(*refs, **static), out_shape=outs, in_...]
    ppermute x7 -> x3, starting transfers between devices: 9.04 us -> 2.63 us  [per_device(): incoming = lax.ppermute(result[0], 'section', pairs)]
  transfers between devices with their start and end apart: 21 -> 3, of which waited for: 21 -> 1; matrix products, arithmetic and copies ran while one was open for 10% -> 0% of each run, Pallas kernels for 0% -> 0%
where the time goes in v2:
time: 132 us; the launch traced here: 131 us
  blocking collectives  98.4 us (75%)
  waiting for transfers between devices  21.7 us (16%)
  Pallas kernels  6.66 us (5%)
  starting transfers between devices  2.63 us (2%)
  local copies, waits for them, and re-layouts  1.61 us (1%)
    all_to_all x8, blocking collectives, exchange(): lax.all_to_all(array, 'expert', split_axis=0, concat_axis=0, tiled=True)  98.4 us
    ppermute x3, waiting for transfers between devices, per_device(): incoming = lax.ppermute(result[0], 'section', pairs)  21.7 us
    pallas_call x12, Pallas kernels, call(): pl.pallas_call(lambda *refs: kernel(*refs, **static), out_shape=outs, in_...  6.66 us
  transfers between devices with their start and end apart: 3, of which 1 were waited for; matrix products, arithmetic and copies ran while one was open for 0% of the time, Pallas kernels for 0%

profile of v2, /device:TPU:24, one launch (start us, length us, event | category | flops | bytes accessed | tf_op | source)
XLA Modules:
  0.0 131.1 jit_solution(3393198646395623314)
XLA Ops:
  0.0 0.9 copy-done.3
  0.9 0.7 copy-done.5
  1.6 0.5 start.1
  2.1 13.5 %all_to_all.88 = bf16[8,32,1024]{2,1,0:T(8,128)(2,1)S(1)} all-to-all(bf16[8,32,1024]{2,1,0:T(8,128)(2,1)S(1)} %bitcast.32), channel_id=1, replica_groups=mesh['section'=4,'expert'=8] {'expert'}, dimensions={0} | all-to-all | bytes 1048576 | tf_op jit(solution)/shard_map/all_to_all | solution.py:204
  15.6 12.1 %all_to_all.89 = bf16[8,32,1024]{2,1,0:T(8,128)(2,1)S(1)} all-to-all(bf16[8,32,1024]{2,1,0:T(8,128)(2,1)S(1)} %bitcast.37), channel_id=1, replica_groups=mesh['section'=4,'expert'=8] {'expert'}, dimensions={0} | all-to-all | bytes 1048576 | tf_op jit(solution)/shard_map/all_to_all | solution.py:204
  27.7 0.2 combine.4
  28.0 0.7 collective-permute-start
  28.7 0.0 copy-start.6
  28.7 0.4 prepare.3
  29.1 12.1 %all_to_all.90 = bf16[8,32,1024]{2,1,0:T(8,128)(2,1)S(1)} all-to-all(bf16[8,32,1024]{2,1,0:T(8,128)(2,1)S(1)} %bitcast.38), channel_id=1, replica_groups=mesh['section'=4,'expert'=8] {'expert'}, dimensions={0} | all-to-all | bytes 1048576 | tf_op jit(solution)/shard_map/all_to_all | solution.py:204
  41.2 12.1 %all_to_all.91 = bf16[8,32,1024]{2,1,0:T(8,128)(2,1)S(1)} all-to-all(bf16[8,32,1024]{2,1,0:T(8,128)(2,1)S(1)} %bitcast.39), channel_id=1, replica_groups=mesh['section'=4,'expert'=8] {'expert'}, dimensions={0} | all-to-all | bytes 1048576 | tf_op jit(solution)/shard_map/all_to_all | solution.py:204
  53.3 0.2 combine.5
  53.6 0.7 collective-permute-start.1
  54.3 0.4 prepare.4
  54.6 12.1 %all_to_all.92 = bf16[8,32,1024]{2,1,0:T(8,128)(2,1)S(1)} all-to-all(bf16[8,32,1024]{2,1,0:T(8,128)(2,1)S(1)} %bitcast.40), channel_id=1, replica_groups=mesh['section'=4,'expert'=8] {'expert'}, dimensions={0} | all-to-all | bytes 1048576 | tf_op jit(solution)/shard_map/all_to_all | solution.py:204
  66.8 12.1 %all_to_all.93 = bf16[8,32,1024]{2,1,0:T(8,128)(2,1)S(1)} all-to-all(bf16[8,32,1024]{2,1,0:T(8,128)(2,1)S(1)} %bitcast.41), channel_id=1, replica_groups=mesh['section'=4,'expert'=8] {'expert'}, dimensions={0} | all-to-all | bytes 1048576 | tf_op jit(solution)/shard_map/all_to_all | solution.py:204
  78.9 0.2 combine.6
  79.1 1.3 collective-permute-start.2
  80.4 21.6 %collective-permute-done.2.refs_1_ = bf16[1,64,1024]{2,1,0:T(8,128)(2,1)S(1)} collective-permute-done((bf16[1,64,1024]{2,1,0:T(8,128)(2,1)S(1)}, bf16[1,64,1024]{2,1,0:T(8,128)(2,1)S(1)}, u32[]{:S(2)}, u32[]{:S(2)}) %collective-permute-start.2) | collective-permute-done | bytes 131104 | tf_op jit(solution)/shard_map/ppermute | solution.py:246
  102.1 0.4 prepare.5
  102.5 12.1 %all_to_all.94 = bf16[8,32,1024]{2,1,0:T(8,128)(2,1)S(1)} all-to-all(bf16[8,32,1024]{2,1,0:T(8,128)(2,1)S(1)} %bitcast.30), channel_id=1, replica_groups=mesh['section'=4,'expert'=8] {'expert'}, dimensions={0} | all-to-all | bytes 1048576 | tf_op jit(solution)/shard_map/all_to_all | solution.py:204
  114.6 3.4 %expert.7 = (bf16[256,1024]{1,0:T(8,128)(2,1)S(1)}, bf16[1,128,256]{2,1,0:T(8,128)(2,1)S(1)}) custom-call(s32[1]{0:T(128)} %bitcast.refs_0_, bf16[256,1024]{1,0:T(8,128)(2,1)S(1)} %bitcast.31, bf16[1024,1792]{1,0:T(8,128)(2,1)S(1)} %bitcast.45, bf16[1024,1792]{1,0:T(8,128)(2,1)S(1)} %bitcast.49, bf16[1792,1024]{1,0:T(8,128)(2,1)S(1)} %bitcast.53, ...), custom_call_target="tpu_custom_call" | custom-call | flops 10000000000 | bytes 100000000 | tf_op jit(solution)/shard_map/expert/pallas_call | solution.py:189
  118.0 12.1 %all_to_all.95 = bf16[8,32,1024]{2,1,0:T(8,128)(2,1)S(1)} all-to-all(bf16[8,32,1024]{2,1,0:T(8,128)(2,1)S(1)} %bitcast.35), channel_id=1, replica_groups=mesh['section'=4,'expert'=8] {'expert'}, dimensions={0} | all-to-all | bytes 1048576 | tf_op jit(solution)/shard_map/all_to_all | solution.py:204
  130.2 0.9 combine.7
  (16 shorter events, 0.0 us)
Async XLA Ops:
  0.0 0.9 copy-start.3
  0.9 0.7 copy-start.5
  1.6 14.0 %copy-start = (bf16[1,1,1024,1792]{3,2,1,0:T(8,128)(2,1)S(1)}, bf16[1,1,1024,1792]{3,2,1,0:T(8,128)(2,1)}, u32[]{:S(2)}) copy-start(bf16[1,1,1024,1792]{3,2,1,0:T(8,128)(2,1)} %param.9) | copy-start | bytes 11010052
  1.6 14.0 %copy-start.1 = (bf16[1,1,1024,1792]{3,2,1,0:T(8,128)(2,1)S(1)}, bf16[1,1,1024,1792]{3,2,1,0:T(8,128)(2,1)}, u32[]{:S(2)}) copy-start(bf16[1,1,1024,1792]{3,2,1,0:T(8,128)(2,1)} %param.10) | copy-start | bytes 11010052
  1.6 14.0 %copy-start.2 = (bf16[1,1,1792,1024]{3,2,1,0:T(8,128)(2,1)S(1)}, bf16[1,1,1792,1024]{3,2,1,0:T(8,128)(2,1)}, u32[]{:S(2)}) copy-start(bf16[1,1,1792,1024]{3,2,1,0:T(8,128)(2,1)} %param.11) | copy-start | bytes 11010052
  1.6 14.0 %copy-start.4 = (f32[1,1,1024,8]{2,3,1,0:T(8,128)S(1)}, f32[1,1,1024,8]{2,3,1,0:T(8,128)}, u32[]{:S(2)}) copy-start(f32[1,1,1024,8]{2,3,1,0:T(8,128)} %param.8) | copy-start | bytes 98308
  28.0 0.7 collective-permute-start
  28.7 12.5 %copy-start.6 = (s32[1,4,1,16,2]{3,4,2,1,0:T(2,128)S(1)}, s32[1,4,1,16,2]{3,4,2,1,0:T(2,128)}, u32[]{:S(2)}) copy-start(s32[1,4,1,16,2]{3,4,2,1,0:T(2,128)} %param.7) | copy-start | bytes 1540
  53.6 0.7 collective-permute-start.1
  79.1 22.9 %collective-permute-start.2 = (bf16[1,64,1024]{2,1,0:T(8,128)(2,1)S(1)}, bf16[1,64,1024]{2,1,0:T(8,128)(2,1)S(1)}, u32[]{:S(2)}, u32[]{:S(2)}) collective-permute-start(bf16[1,64,1024]{2,1,0:T(8,128)(2,1)S(1)} %get-tuple-element.47), channel_id=1, source_target_pairs={{16,24},{17,25},{18,26},{19,27},{20,28},{21,29},{22,30},{23,31}} | collective-permute-start | bytes 393224 | tf_op jit(solution)/shard_map/ppermute | solution.py:246
